TPU v7x, 256 devices: a whole 4x4x8 slice. The times are simulated.
256 devices in a mesh: replica: 8 (over y, core), shard: 32 (over x, z).
Axes of the slice: x: 4, y: 4, z: 8, core: 2. Of those that a mesh axis runs over, the one named last changes fastest.
Arguments:
- deltas: bfloat16 [8, 64, 128, 6144], P('replica', None, 'shard')
- block_list: int32 [8, 64], replicated, may hold values from -1 to 127, as said below
- hosting: int32 [8, 16, 8], replicated, may hold values from 0 to 1, as said below
- counts: int32 [8, 128], replicated, may hold values from 1 to 63
- params: float32 [128, 128, 6144], P('shard', 'replica'), may hold values from -6 to 6
- momentum: float32 [128, 128, 6144], P('shard', 'replica'), may hold values from -4 to 4
Outputs:
- new_params: float32 [128, 128, 6144], P('shard', 'replica')
- new_momentum: float32 [128, 128, 6144], P('shard', 'replica')
- host_params: bfloat16 [8, 64, 128, 6144], P('replica', None, 'shard')
Inputs may be any that keep to these rules, and one draw needn't show every extreme that they name: `block_list`: row r lists, each once and in any order, the blocks whose parameters replica r holds, with -1 in the other entries; block b is owned by shard b // 4, and at most 2 listed blocks of one row have the same owner. `hosting`: 1 only for blocks that appear in the replica's row of block_list.
All inputs are finite; a program needn't handle non-finite values.
Results may differ from a plain program's by a relative error of at most 0.001.
Values may be sent and summed in bfloat16 or wider, within the bound.
A program may use at most 128 MiB of HBM per device.

v0:
```python
import math
import jax
import jax.numpy as jnp
from jax import lax
from jax.sharding import Mesh
from jax.sharding import PartitionSpec as P

D = 6144
ROWS = 128
REPLICA = ("replica_0", "replica_1")
SHARD = ("shard_0", "shard_1")
REPLICA_SHARD = ("replica_0", "replica_1", "shard_0", "shard_1")
decay_rate = 0.9
outer_rate = 0.7
limit_ratio = 0.1


def by_axis(shard, axes):
    for axis in axes:
        shard = lax.psum(shard, axis)
    return shard


def slot_placement(block_lists, owned_count, capacity, shard_count):
    listed = block_lists >= 0
    owner_shard = jnp.where(listed, block_lists // owned_count, -1)
    same_owner = (owner_shard[:, :, None] == jnp.arange(shard_count)[None, None, :]).astype(
        jnp.int32
    )
    owner_rank = jnp.sum(jnp.cumsum(same_owner, axis=1) * same_owner, axis=2) - 1
    return jnp.where(listed, owner_shard * capacity + owner_rank, -1)


def per_device(deltas, block_list, hosting, counts, params, momentum):
    replicas = lax.axis_size(REPLICA)
    shard_count = lax.axis_size(SHARD)
    replica_index = lax.axis_index(REPLICA)
    shard_index = lax.axis_index(SHARD)
    slot_count = block_list.shape[1]
    capacity = slot_count // shard_count
    block_count = counts.shape[1]
    owned_count = block_count // shard_count
    local_rows = deltas.shape[2]
    owner_rows = params.shape[1]
    flat_local = deltas[0].reshape(slot_count, local_rows * D)
    weight = hosting.reshape(replicas, block_count) * counts
    totals = jnp.maximum(jnp.sum(weight, axis=0).astype(jnp.float32), 1.0)
    first_owned = shard_index * owned_count
    targets = first_owned + jnp.arange(owned_count)
    own_weight = lax.dynamic_slice_in_dim(weight, first_owned, owned_count, 1)
    own_totals = lax.dynamic_slice_in_dim(totals, first_owned, owned_count, 0)
    placement_all = slot_placement(block_list, owned_count, capacity, shard_count)
    my_place = lax.dynamic_index_in_dim(placement_all, replica_index, 0, keepdims=False)
    packing = (jnp.arange(slot_count)[:, None] == my_place[None, :]).astype(jnp.bfloat16)
    packed = jnp.dot(packing, flat_local, preferred_element_type=jnp.float32).astype(jnp.bfloat16)
    packed = packed.reshape(shard_count, capacity, local_rows, D)
    at_owner = lax.all_to_all(packed, SHARD, split_axis=0, concat_axis=2, tiled=True)
    gathered = lax.all_to_all(at_owner, REPLICA, split_axis=2, concat_axis=0, tiled=True)
    wanted = shard_index * capacity + jnp.arange(capacity)
    select = (placement_all[:, None, :] == wanted[None, :, None]).astype(jnp.int32)
    slot_block = jnp.sum(select * block_list[:, None, :], axis=2) - (1 - jnp.sum(select, axis=2))
    matches = slot_block[:, :, None] == targets[None, None, :]
    slot_weight = jnp.where(matches, own_weight[:, None, :], 0)
    mixing = slot_weight.reshape(replicas * capacity, owned_count).astype(jnp.bfloat16)
    summed = jnp.einsum(
        "sj,sx->jx",
        mixing,
        gathered.reshape(replicas * capacity, owner_rows * D),
        preferred_element_type=jnp.float32,
    )
    gradient = summed.reshape(owned_count, owner_rows, D) / own_totals[:, None, None]
    square_sum = by_axis(jnp.sum(gradient * gradient), REPLICA_SHARD)
    limit = limit_ratio * math.sqrt(block_count * ROWS * D)
    clip_factor = jnp.minimum(1.0, limit / jnp.sqrt(square_sum + 1e-06))
    scaled = clip_factor * gradient
    new_momentum = decay_rate * momentum + scaled
    new_params = params - outer_rate * (scaled + decay_rate * new_momentum)
    hosted = new_params.astype(jnp.bfloat16)
    sending = jnp.einsum(
        "rcj,jx->rcx",
        matches.astype(jnp.bfloat16),
        hosted.reshape(owned_count, owner_rows * D),
        preferred_element_type=jnp.float32,
    ).astype(jnp.bfloat16)
    sending = sending.reshape(replicas, capacity, owner_rows, D)
    returned = lax.all_to_all(
        lax.all_to_all(sending, REPLICA, split_axis=0, concat_axis=2, tiled=True),
        SHARD,
        split_axis=2,
        concat_axis=0,
        tiled=True,
    )
    host_rows = jnp.einsum(
        "pk,px->kx",
        packing,
        returned.reshape(slot_count, local_rows * D),
        preferred_element_type=jnp.float32,
    ).astype(jnp.bfloat16)
    return (new_params, new_momentum, host_rows.reshape(1, slot_count, local_rows, D))


def solution(mesh):
    finer = Mesh(mesh.devices.reshape(4, 2, 4, 8), ("replica_0", "replica_1", "shard_0", "shard_1"))
    in_specs = (
        P(REPLICA, None, SHARD, None),
        P(),
        P(),
        P(),
        P(SHARD, REPLICA, None),
        P(SHARD, REPLICA, None),
    )
    out_specs = (P(SHARD, REPLICA, None), P(SHARD, REPLICA, None), P(REPLICA, None, SHARD, None))
    return jax.shard_map(
        per_device, mesh=finer, in_specs=in_specs, out_specs=out_specs, check_vma=False
    )
```

profile of v0, /device:TPU:8, one launch (start us, length us, event | category | flops | bytes accessed | tf_op | source)
XLA Modules:
  0.0 331.8 jit_solution(15116666798434059264)
XLA Ops:
  0.6 0.8 copy.72
  1.4 1.3 fusion.15
  2.8 3.7 %copy.97 = bf16[8,8,4,6144]{3,1,2,0:T(8,128)(2,1)S(1)} copy(bf16[8,8,4,6144]{3,2,1,0:T(4,128)(2,1)} %bitcast.58) | data formatting | bytes 6291456
  6.5 0.2 dynamic-slice_reduce_fusion
  6.7 2.6 convolution_convert_fusion.2
  9.3 4.1 %reshape.102 = bf16[32,2,4,6144]{3,2,1,0:T(4,128)(2,1)S(1)} reshape(bf16[64,24576]{1,0:T(8,128)(2,1)} %convolution_convert_fusion.2) | data formatting | bytes 6291456 | tf_op jit(solution)/shard_map/reshape | solution.py:56
  13.5 3.2 copy.80
  16.7 84.9 %all_to_all.66 = bf16[32,2,4,6144]{3,1,2,0:T(2,128)(2,1)} all-to-all(bf16[32,2,4,6144]{3,1,2,0:T(2,128)(2,1)S(1)} %copy.80), channel_id=1, replica_groups=mesh['replica_0'=4,'replica_1'=2,'shard_0'=4,'shard_1'=8] {'shard_0','sh..., dimensions={0} | all-to-all | bytes 6291456 | tf_op jit(solution)/shard_map/all_to_all | solution.py:57
  101.6 5.0 %all-to-all-start.1 = ((bf16[1,2,128,6144]{3,1,0,2:T(2,128)(2,1)}), bf16[1,2,128,6144]{3,1,0,2:T(2,128)(2,1)S(1)}, u32[]{:S(2)}, u32[]{:S(2)}) async-start(bf16[1,2,128,6144]{3,1,0,2:T(2,128)(2,1)} %bitcast.50), calls=%async_computation.1 | async-start | bytes 6291456 | tf_op jit(solution)/shard_map/all_to_all | solution.py:58
  106.7 0.2 fusion.11
  107.1 0.1 reshape.101
  107.4 36.1 %all-to-all-done.1 = bf16[1,2,128,6144]{3,1,0,2:T(2,128)(2,1)S(1)} async-done(((bf16[1,2,128,6144]{3,1,0,2:T(2,128)(2,1)}), bf16[1,2,128,6144]{3,1,0,2:T(2,128)(2,1)S(1)}, u32[]{:S(2)}, u32[]{:S(2)}) %all-to-all-start.1) | async-done | bytes 3145760 | tf_op jit(solution)/shard_map/all_to_all | solution.py:58
  143.5 1.1 copy.82
  144.7 5.2 %multiply_reduce_fusion = (f32[]{:T(128)}, f32[4,16,6144]{2,0,1:T(4,128)}) fusion(f32[4]{0:T(128)S(1)} %dynamic_slice.12, bf16[16,4,1]{1,0,2:T(8,128)(2,1)S(1)} %bitcast.60, bf16[2,8,16,6144]{3,2,1,0:T(8,128)(2,1)S(1)} %bitcast.59), kind=kOutput, calls=%fused_computation.9 | convolution fusion | flops 13762559 | bytes 4718740 | tf_op jit(solution)/shard_map/sj,sx->jx/dot_general | solution.py:65
  149.8 9.8 %psum.28 = f32[]{:T(128)} all-reduce(f32[]{:T(128)} %get-tuple-element.27), channel_id=1, replica_groups=mesh['replica_0'=4,'replica_1'=2,'shard_0'=4,'shard_1'=8] {'replica_0'}, use_global_device_ids=true, to_apply=%region_6.7 | all-reduce | flops 1 | bytes 8 | tf_op jit(solution)/shard_map/psum | solution.py:20
  159.6 3.1 psum.29
  162.7 9.1 %psum.30 = f32[]{:T(128)} all-reduce(f32[]{:T(128)} %psum.29), channel_id=1, replica_groups=mesh['replica_0'=4,'replica_1'=2,'shard_0'=4,'shard_1'=8] {'shard_0'}, use_global_device_ids=true, to_apply=%region_8.9 | all-reduce | flops 1 | bytes 8 | tf_op jit(solution)/shard_map/psum | solution.py:20
  171.8 16.8 %psum.31 = f32[]{:T(128)} all-reduce(f32[]{:T(128)} %psum.30), channel_id=1, replica_groups=mesh['replica_0'=4,'replica_1'=2,'shard_0'=4,'shard_1'=8] {'shard_1'}, use_global_device_ids=true, to_apply=%region_9.10 | all-reduce | flops 1 | bytes 8 | tf_op jit(solution)/shard_map/psum | solution.py:20
  189.4 6.0 %fusion.13 = (bf16[4,16,6144]{2,0,1:T(4,128)(2,1)S(1)}, f32[4,16,6144]{2,0,1:T(4,128)}, f32[4,16,6144]{2,0,1:T(4,128)}) fusion(f32[4,16,6144]{2,1,0:T(8,128)S(1)} %copy-done.1, f32[4,16,6144]{2,0,1:T(4,128)} %get-tuple-element.28, f32[]{:T(128)S(6)} %min.3, f32[4,16,6144]{2,1,0:T(8,128)S(1)} %copy-done.2), kind=kLoop, calls=%fused_computation.40 | loop fusion | flops 3145728 | bytes 8650756 | tf_op jit(solution)/shard_map/convert_element_type | solution.py:78
  195.3 1.0 convolution_convert_fusion
  196.3 1.7 copy.88
  198.0 41.0 %all_to_all.67 = bf16[8,2,16,6144]{3,2,1,0:T(8,128)(2,1)S(1)} all-to-all(bf16[8,2,16,6144]{3,2,1,0:T(8,128)(2,1)S(1)} %copy.88), channel_id=1, replica_groups=mesh['replica_0'=4,'replica_1'=2,'shard_0'=4,'shard_1'=8] {'replica_0','..., dimensions={0} | all-to-all | bytes 6291456 | tf_op jit(solution)/shard_map/all_to_all | solution.py:87
  239.0 0.2 copy.89
  239.2 4.9 %copy.90 = bf16[1,2,128,6144]{3,1,0,2:T(2,128)(2,1)} copy(bf16[1,2,128,6144]{3,2,1,0:T(8,128)(2,1)S(1)} %bitcast.55) | data formatting | bytes 6291456 | tf_op jit(solution)/shard_map/all_to_all | solution.py:87
  244.1 5.3 %all-to-all-start.3 = ((bf16[1,2,128,6144]{3,1,0,2:T(2,128)(2,1)}), bf16[1,2,128,6144]{3,1,0,2:T(2,128)(2,1)S(1)}, u32[]{:S(2)}, u32[]{:S(2)}) async-start(bf16[1,2,128,6144]{3,1,0,2:T(2,128)(2,1)} %copy.90), calls=%async_computation.3 | async-start | bytes 6291456 | tf_op jit(solution)/shard_map/all_to_all | solution.py:86
  249.5 3.6 %copy.92 = f32[4,16,6144]{2,1,0:T(8,128)} copy(f32[4,16,6144]{2,0,1:T(4,128)} %get-tuple-element.21) | data formatting | bytes 3145728
  253.1 2.1 copy.93
  255.1 68.6 %all-to-all-done.3 = bf16[1,2,128,6144]{3,1,0,2:T(2,128)(2,1)S(1)} async-done(((bf16[1,2,128,6144]{3,1,0,2:T(2,128)(2,1)}), bf16[1,2,128,6144]{3,1,0,2:T(2,128)(2,1)S(1)}, u32[]{:S(2)}, u32[]{:S(2)}) %all-to-all-start.3) | async-done | bytes 3145760 | tf_op jit(solution)/shard_map/all_to_all | solution.py:86
  323.7 1.6 copy.91
  325.3 1.8 copy.99
  327.2 1.0 convolution_convert_fusion.1
  328.2 3.6 %reshape.107 = bf16[1,64,4,6144]{3,2,1,0:T(4,128)(2,1)} reshape(bf16[64,24576]{1,0:T(8,128)(2,1)S(1)} %convolution_convert_fusion.1) | data formatting | bytes 6291456 | tf_op jit(solution)/shard_map/reshape | solution.py:99
  (25 shorter events, 0.6 us)
Async XLA Ops:
  101.5 5.1 %copy-start.4 = (s32[8,64]{1,0:T(8,128)S(1)}, s32[8,64]{1,0:T(8,128)}, u32[]{:S(2)}) copy-start(s32[8,64]{1,0:T(8,128)} %param.7) | copy-start | bytes 6148
  101.5 5.4 %copy-start.3 = (s32[8,16,8]{1,2,0:T(8,128)S(1)}, s32[8,16,8]{1,2,0:T(8,128)}, u32[]{:S(2)}) copy-start(s32[8,16,8]{1,2,0:T(8,128)} %param.8) | copy-start | bytes 12292
  101.6 5.6 %copy-start.5 = (s32[8,128]{1,0:T(8,128)S(1)}, s32[8,128]{1,0:T(8,128)}, u32[]{:S(2)}) copy-start(s32[8,128]{1,0:T(8,128)} %param.9) | copy-start | bytes 12292
  101.6 42.0 %all-to-all-start.1 = ((bf16[1,2,128,6144]{3,1,0,2:T(2,128)(2,1)}), bf16[1,2,128,6144]{3,1,0,2:T(2,128)(2,1)S(1)}, u32[]{:S(2)}, u32[]{:S(2)}) async-start(bf16[1,2,128,6144]{3,1,0,2:T(2,128)(2,1)} %bitcast.50), calls=%async_computation.1 | async-start | bytes 6291456 | tf_op jit(solution)/shard_map/all_to_all | solution.py:58
  144.6 44.7 %copy-start.1 = (f32[4,16,6144]{2,1,0:T(8,128)S(1)}, f32[4,16,6144]{2,1,0:T(8,128)}, u32[]{:S(2)}) copy-start(f32[4,16,6144]{2,1,0:T(8,128)} %param.11) | copy-start | bytes 4718596
  144.6 44.7 %copy-start.2 = (f32[4,16,6144]{2,1,0:T(8,128)S(1)}, f32[4,16,6144]{2,1,0:T(8,128)}, u32[]{:S(2)}) copy-start(f32[4,16,6144]{2,1,0:T(8,128)} %param.10) | copy-start | bytes 4718596
  244.1 79.6 %all-to-all-start.3 = ((bf16[1,2,128,6144]{3,1,0,2:T(2,128)(2,1)}), bf16[1,2,128,6144]{3,1,0,2:T(2,128)(2,1)S(1)}, u32[]{:S(2)}, u32[]{:S(2)}) async-start(bf16[1,2,128,6144]{3,1,0,2:T(2,128)(2,1)} %copy.90), calls=%async_computation.3 | async-start | bytes 6291456 | tf_op jit(solution)/shard_map/all_to_all | solution.py:86
  249.5 3.6 %copy-start = (f32[4,16,6144]{2,0,1:T(4,128)S(1)}, f32[4,16,6144]{2,0,1:T(4,128)}, u32[]{:S(2)}) copy-start(f32[4,16,6144]{2,0,1:T(4,128)} %get-tuple-element.26) | copy-start | bytes 4718596
where the time goes:
time: 332 us
  blocking collectives  165 us (50%)
  waiting for transfers between devices  105 us (32%)
  local copies, waits for them, and re-layouts  33.1 us (10%)
  starting transfers between devices  10.3 us (3%)
  matrix products  9.8 us (3%)
  other arithmetic  7.66 us (2%)
    all_to_all x1, blocking collectives, per_device(): lax.all_to_all(packed, SHARD, split_axis=0, concat_axis=2, tiled=True)  84.9 us
    all_to_all x1, waiting for transfers between devices, per_device(): lax.all_to_all(lax.all_to_all(sending, REPLICA, split_axis=0, concat_axis...  68.6 us
    all_to_all x1, blocking collectives, per_device(): lax.all_to_all(sending, REPLICA, split_axis=0, concat_axis=2, tiled=True)  41 us
    psum x4, blocking collectives, by_axis(): shard = lax.psum(shard, axis)  38.8 us
    all_to_all x1, waiting for transfers between devices, per_device(): lax.all_to_all(at_owner, REPLICA, split_axis=2, concat_axis=0, tiled=True)  36.1 us
    unnamed x18, local copies, waits for them, and re-layouts  12 us
    reshape x2, local copies, waits for them, and re-layouts, per_device(): packed = packed.reshape(shard_count, capacity, local_rows, D)  7.37 us
  transfers between devices with their start and end apart: 2, of which 2 were waited for; matrix products, arithmetic and copies ran while one was open for 2% of the time, Pallas kernels for 0%

commit v1 on v0

--- a/solution.py
+++ b/solution.py
@@ -17,7 +17,8 @@
 
 def by_axis(shard, axes):
     for axis in axes:
-        shard = lax.psum(shard, axis)
+        pieces = lax.all_gather(shard, axis, axis=0, tiled=False)
+        shard = pieces.sum(axis=0)
     return shard
 
 

time: 332 us -> 340 us (1.024)
  local copies, waits for them, and re-layouts: 33.1 us -> 41 us
    psum x4 -> x0, blocking collectives: 38.8 us -> none  [by_axis(): shard = lax.psum(shard, axis)]
    unnamed x0 -> x4, blocking collectives: none -> 36.3 us
    unnamed x18 -> x38, local copies, waits for them, and re-layouts: 12 us -> 20 us
where the time goes in v1:
time: 340 us; the launch traced here: 339 us
  blocking collectives  162 us (48%)
  waiting for transfers between devices  104 us (31%)
  local copies, waits for them, and re-layouts  41 us (12%)
  starting transfers between devices  10.4 us (3%)
  other arithmetic  10.1 us (3%)
  matrix products  9.8 us (3%)
    all_to_all x1, blocking collectives, per_device(): lax.all_to_all(packed, SHARD, split_axis=0, concat_axis=2, tiled=True)  84.9 us
    all_to_all x1, waiting for transfers between devices, per_device(): lax.all_to_all(lax.all_to_all(sending, REPLICA, split_axis=0, concat_axis...  68.6 us
    all_to_all x1, blocking collectives, per_device(): lax.all_to_all(sending, REPLICA, split_axis=0, concat_axis=2, tiled=True)  41 us
    unnamed x4, blocking collectives  36.3 us
    all_to_all x1, waiting for transfers between devices, per_device(): lax.all_to_all(at_owner, REPLICA, split_axis=2, concat_axis=0, tiled=True)  35.5 us
    unnamed x38, local copies, waits for them, and re-layouts  20 us
    reshape x2, local copies, waits for them, and re-layouts, per_device(): packed = packed.reshape(shard_count, capacity, local_rows, D)  7.37 us
  transfers between devices with their start and end apart: 2, of which 2 were waited for; matrix products, arithmetic and copies ran while one was open for 2% of the time, Pallas kernels for 0%

profile of v1, /device:TPU:8, one launch (start us, length us, event | category | flops | bytes accessed | tf_op | source)
XLA Modules:
  0.0 339.1 jit_solution(3412133086456763877)
XLA Ops:
  0.6 0.8 copy.72
  1.4 1.3 fusion.15
  2.8 3.7 %copy.97 = bf16[8,8,4,6144]{3,1,2,0:T(8,128)(2,1)S(1)} copy(bf16[8,8,4,6144]{3,2,1,0:T(4,128)(2,1)} %bitcast.66) | data formatting | bytes 6291456
  6.7 2.6 convolution_convert_fusion.2
  9.3 4.1 %reshape.102 = bf16[32,2,4,6144]{3,2,1,0:T(4,128)(2,1)S(1)} reshape(bf16[64,24576]{1,0:T(8,128)(2,1)} %convolution_convert_fusion.2) | data formatting | bytes 6291456 | tf_op jit(solution)/shard_map/reshape | solution.py:57
  13.5 3.2 copy.80
  16.7 84.9 %all_to_all.66 = bf16[32,2,4,6144]{3,1,2,0:T(2,128)(2,1)} all-to-all(bf16[32,2,4,6144]{3,1,2,0:T(2,128)(2,1)S(1)} %copy.80), channel_id=1, replica_groups=mesh['replica_0'=4,'replica_1'=2,'shard_0'=4,'shard_1'=8] {'shard_0','sh..., dimensions={0} | all-to-all | bytes 6291456 | tf_op jit(solution)/shard_map/all_to_all | solution.py:58
  101.6 5.1 %all-to-all-start.1 = ((bf16[1,2,128,6144]{3,1,0,2:T(2,128)(2,1)}), bf16[1,2,128,6144]{3,1,0,2:T(2,128)(2,1)S(1)}, u32[]{:S(2)}, u32[]{:S(2)}) async-start(bf16[1,2,128,6144]{3,1,0,2:T(2,128)(2,1)} %bitcast.58), calls=%async_computation.1 | async-start | bytes 6291456 | tf_op jit(solution)/shard_map/all_to_all | solution.py:59
  108.0 35.5 %all-to-all-done.1 = bf16[1,2,128,6144]{3,1,0,2:T(2,128)(2,1)S(1)} async-done(((bf16[1,2,128,6144]{3,1,0,2:T(2,128)(2,1)}), bf16[1,2,128,6144]{3,1,0,2:T(2,128)(2,1)S(1)}, u32[]{:S(2)}, u32[]{:S(2)}) %all-to-all-start.1) | async-done | bytes 3145760 | tf_op jit(solution)/shard_map/all_to_all | solution.py:59
  143.6 1.1 copy.82
  144.7 5.2 %multiply_reduce_fusion = (f32[]{:T(128)}, f32[4,16,6144]{2,0,1:T(4,128)}) fusion(f32[4]{0:T(128)S(1)} %dynamic_slice.12, bf16[16,4,1]{1,0,2:T(8,128)(2,1)S(1)} %bitcast.68, bf16[2,8,16,6144]{3,2,1,0:T(8,128)(2,1)S(1)} %bitcast.67), kind=kOutput, calls=%fused_computation.9 | convolution fusion | flops 13762559 | bytes 4718740 | tf_op jit(solution)/shard_map/sj,sx->jx/dot_general | solution.py:66
  149.9 1.4 dynamic-update-slice
  151.9 9.2 %all-reduce = f32[4]{0:T(128)S(1)} all-reduce(f32[4]{0:T(128)S(1)} %dynamic-update-slice), channel_id=1, replica_groups=mesh['replica_0'=4,'replica_1'=2,'shard_0'=4,'shard_1'=8] {'replica_0'}, use_global_device_ids=true, to_apply=%add | all-reduce | flops 4 | bytes 32
  161.6 1.4 dynamic-update-slice.1
  163.6 2.4 all-reduce.1
  166.7 1.4 dynamic-update-slice.2
  168.7 8.5 %all-reduce.2 = f32[4]{0:T(128)S(1)} all-reduce(f32[4]{0:T(128)S(1)} %dynamic-update-slice.2), channel_id=1, replica_groups=mesh['replica_0'=4,'replica_1'=2,'shard_0'=4,'shard_1'=8] {'shard_0'}, use_global_device_ids=true, to_apply=%add.2 | all-reduce | flops 4 | bytes 32
  177.8 1.4 dynamic-update-slice.3
  179.2 16.2 %all-reduce.3 = f32[8]{0:T(128)S(1)} all-reduce(f32[8]{0:T(128)S(1)} %dynamic-update-slice.3), channel_id=1, replica_groups=mesh['replica_0'=4,'replica_1'=2,'shard_0'=4,'shard_1'=8] {'shard_1'}, use_global_device_ids=true, to_apply=%add.3 | all-reduce | flops 8 | bytes 64
  196.7 6.0 %fusion.13 = (bf16[4,16,6144]{2,0,1:T(4,128)(2,1)S(1)}, f32[4,16,6144]{2,0,1:T(4,128)}, f32[4,16,6144]{2,0,1:T(4,128)}) fusion(f32[4,16,6144]{2,1,0:T(8,128)S(1)} %copy-done.1, f32[4,16,6144]{2,0,1:T(4,128)} %get-tuple-element.28, f32[]{:T(128)S(6)} %min.3, f32[4,16,6144]{2,1,0:T(8,128)S(1)} %copy-done.2), kind=kLoop, calls=%fused_computation.40 | loop fusion | flops 3145728 | bytes 8650756 | tf_op jit(solution)/shard_map/convert_element_type | solution.py:79
  202.6 1.0 convolution_convert_fusion
  203.6 1.7 copy.88
  205.3 41.0 %all_to_all.67 = bf16[8,2,16,6144]{3,2,1,0:T(8,128)(2,1)S(1)} all-to-all(bf16[8,2,16,6144]{3,2,1,0:T(8,128)(2,1)S(1)} %copy.88), channel_id=1, replica_groups=mesh['replica_0'=4,'replica_1'=2,'shard_0'=4,'shard_1'=8] {'replica_0','..., dimensions={0} | all-to-all | bytes 6291456 | tf_op jit(solution)/shard_map/all_to_all | solution.py:88
  246.6 4.9 %copy.90 = bf16[1,2,128,6144]{3,1,0,2:T(2,128)(2,1)} copy(bf16[1,2,128,6144]{3,2,1,0:T(8,128)(2,1)S(1)} %bitcast.63) | data formatting | bytes 6291456 | tf_op jit(solution)/shard_map/all_to_all | solution.py:88
  251.5 5.3 %all-to-all-start.3 = ((bf16[1,2,128,6144]{3,1,0,2:T(2,128)(2,1)}), bf16[1,2,128,6144]{3,1,0,2:T(2,128)(2,1)S(1)}, u32[]{:S(2)}, u32[]{:S(2)}) async-start(bf16[1,2,128,6144]{3,1,0,2:T(2,128)(2,1)} %copy.90), calls=%async_computation.3 | async-start | bytes 6291456 | tf_op jit(solution)/shard_map/all_to_all | solution.py:87
  256.8 3.6 %copy.92 = f32[4,16,6144]{2,1,0:T(8,128)} copy(f32[4,16,6144]{2,0,1:T(4,128)} %get-tuple-element.21) | data formatting | bytes 3145728
  260.4 2.1 copy.93
  262.4 68.6 %all-to-all-done.3 = bf16[1,2,128,6144]{3,1,0,2:T(2,128)(2,1)S(1)} async-done(((bf16[1,2,128,6144]{3,1,0,2:T(2,128)(2,1)}), bf16[1,2,128,6144]{3,1,0,2:T(2,128)(2,1)S(1)}, u32[]{:S(2)}, u32[]{:S(2)}) %all-to-all-start.3) | async-done | bytes 3145760 | tf_op jit(solution)/shard_map/all_to_all | solution.py:87
  331.0 1.6 copy.91
  332.6 1.8 copy.99
  334.5 1.0 convolution_convert_fusion.1
  335.5 3.6 %reshape.107 = bf16[1,64,4,6144]{3,2,1,0:T(4,128)(2,1)} reshape(bf16[64,24576]{1,0:T(8,128)(2,1)S(1)} %convolution_convert_fusion.1) | data formatting | bytes 6291456 | tf_op jit(solution)/shard_map/reshape | solution.py:100
  (49 shorter events, 6.0 us)
Async XLA Ops:
  101.5 5.1 %copy-start.4 = (s32[8,64]{1,0:T(8,128)S(1)}, s32[8,64]{1,0:T(8,128)}, u32[]{:S(2)}) copy-start(s32[8,64]{1,0:T(8,128)} %param.7) | copy-start | bytes 6148
  101.5 5.4 %copy-start.3 = (s32[8,16,8]{1,2,0:T(8,128)S(1)}, s32[8,16,8]{1,2,0:T(8,128)}, u32[]{:S(2)}) copy-start(s32[8,16,8]{1,2,0:T(8,128)} %param.8) | copy-start | bytes 12292
  101.6 5.6 %copy-start.9 = (u32[256]{0:T(256)S(1)}, u32[256]{0:T(256)}, u32[]{:S(2)}) copy-start(u32[256]{0:T(256)} %constant.74) | copy-start | bytes 3076
  101.6 6.2 %copy-start.5 = (s32[8,128]{1,0:T(8,128)S(1)}, s32[8,128]{1,0:T(8,128)}, u32[]{:S(2)}) copy-start(s32[8,128]{1,0:T(8,128)} %param.9) | copy-start | bytes 12292
  101.6 42.0 %all-to-all-start.1 = ((bf16[1,2,128,6144]{3,1,0,2:T(2,128)(2,1)}), bf16[1,2,128,6144]{3,1,0,2:T(2,128)(2,1)S(1)}, u32[]{:S(2)}, u32[]{:S(2)}) async-start(bf16[1,2,128,6144]{3,1,0,2:T(2,128)(2,1)} %bitcast.58), calls=%async_computation.1 | async-start | bytes 6291456 | tf_op jit(solution)/shard_map/all_to_all | solution.py:59
  144.7 6.6 %copy-start.8 = (u32[256]{0:T(256)S(1)}, u32[256]{0:T(256)}, u32[]{:S(2)}) copy-start(u32[256]{0:T(256)} %constant.79) | copy-start | bytes 3076
  144.7 18.4 %copy-start.7 = (u32[256]{0:T(256)S(1)}, u32[256]{0:T(256)}, u32[]{:S(2)}) copy-start(u32[256]{0:T(256)} %constant.84) | copy-start | bytes 3076
  144.7 23.4 %copy-start.6 = (u32[256]{0:T(256)S(1)}, u32[256]{0:T(256)}, u32[]{:S(2)}) copy-start(u32[256]{0:T(256)} %constant.89) | copy-start | bytes 3076
  144.7 52.0 %copy-start.1 = (f32[4,16,6144]{2,1,0:T(8,128)S(1)}, f32[4,16,6144]{2,1,0:T(8,128)}, u32[]{:S(2)}) copy-start(f32[4,16,6144]{2,1,0:T(8,128)} %param.11) | copy-start | bytes 4718596
  144.7 52.0 %copy-start.2 = (f32[4,16,6144]{2,1,0:T(8,128)S(1)}, f32[4,16,6144]{2,1,0:T(8,128)}, u32[]{:S(2)}) copy-start(f32[4,16,6144]{2,1,0:T(8,128)} %param.10) | copy-start | bytes 4718596
  251.5 79.6 %all-to-all-start.3 = ((bf16[1,2,128,6144]{3,1,0,2:T(2,128)(2,1)}), bf16[1,2,128,6144]{3,1,0,2:T(2,128)(2,1)S(1)}, u32[]{:S(2)}, u32[]{:S(2)}) async-start(bf16[1,2,128,6144]{3,1,0,2:T(2,128)(2,1)} %copy.90), calls=%async_computation.3 | async-start | bytes 6291456 | tf_op jit(solution)/shard_map/all_to_all | solution.py:87
  256.8 3.6 %copy-start = (f32[4,16,6144]{2,0,1:T(4,128)S(1)}, f32[4,16,6144]{2,0,1:T(4,128)}, u32[]{:S(2)}) copy-start(f32[4,16,6144]{2,0,1:T(4,128)} %get-tuple-element.26) | copy-start | bytes 4718596
